TPU v7x, 32 devices: a whole 2x2x4 slice. The times are simulated.
32 devices in a mesh: rep: 8 (over y, x, core), tp: 4 (over z).
Axes of the slice: x: 2, y: 2, z: 4, core: 2. Of those that a mesh axis runs over, the one named last changes fastest.
Arguments:
- queries: bfloat16 [2048, 4096], P('rep', 'tp'), may hold values from -120 to 120
- keys_new: bfloat16 [2048, 1024], P('rep', 'tp'), may hold values from -7 to 7
- values_new: bfloat16 [2048, 1024], P('rep', 'tp'), may hold values from -6 to 6
- caches: bfloat16 [16, 2, 4096, 1024], P('rep', None, None, 'tp'), may hold values from -6 to 6
- lengths: int32 [8, 2], replicated, may hold values from 128 to 4096, as said below
- moving: int32 [8], replicated, may hold values from 0 to 1
- destination: int32 [8], replicated, may hold values from 0 to 7, each once
- out_weight: bfloat16 [4096, 4096], P('tp'), may hold values from -0.09375 to 0.09375
Outputs:
- mixed: bfloat16 [2048, 4096], P('rep', 'tp')
- held_cache: bfloat16 [16, 2, 4096, 1024], P('rep', None, None, 'tp')
Inputs may be any that keep to these rules, and one draw needn't show every extreme that they name: `lengths`: multiples of 128; in every draw some slot holds 4096 and some 128. `destination`: each replica receives exactly one failing candidate; it takes the slot that its own failing candidate leaves.
All inputs are finite; a program needn't handle non-finite values.
Results may differ from a plain program's by a relative error of at most 0.014.
Values may be sent and summed in bfloat16 or wider, within the bound.
A program may use at most 64 MiB of HBM per device.

v0:
```python
import jax
import jax.numpy as jnp
from jax import lax
from jax.sharding import PartitionSpec as P

HEAD = 128
masked_score = -1e30
key_block_rows = 512


def attend(query_slot, key_cache, value_cache, length, keys_fresh, values_fresh, block_count):
    span_rows = query_slot.shape[0]
    kv_count = key_cache.shape[1] // HEAD
    group_size = query_slot.shape[1] // (HEAD * kv_count)
    grouped = query_slot.reshape(span_rows, kv_count, group_size, HEAD).transpose(1, 2, 0, 3)
    grouped = grouped.reshape(kv_count, group_size * span_rows, HEAD)
    scale = HEAD ** (-0.5)
    token_of_row = jnp.arange(group_size * span_rows, dtype=jnp.int32) % span_rows

    def absorb(running, key_block, value_block, visible):
        row_max, row_total, weighted = running
        scores = (
            jnp.einsum("gqd,kgd->gqk", grouped, key_block, preferred_element_type=jnp.float32)
            * scale
        )
        scores = jnp.where(visible, scores, masked_score)
        new_max = jnp.maximum(row_max, jnp.max(scores, axis=2))
        rescale = jnp.exp(row_max - new_max)
        weights_block = jnp.where(visible, jnp.exp(scores - new_max[:, :, None]), 0.0)
        row_total = row_total * rescale + jnp.sum(weights_block, axis=2)
        weighted = weighted * rescale[:, :, None] + jnp.einsum(
            "gqk,kgd->gqd",
            weights_block.astype(jnp.bfloat16),
            value_block,
            preferred_element_type=jnp.float32,
        )
        return (new_max, row_total, weighted)

    def cache_step(block_index, running):
        start = block_index * key_block_rows
        key_block = lax.dynamic_slice_in_dim(key_cache, start, key_block_rows, 0).reshape(
            key_block_rows, kv_count, HEAD
        )
        value_block = lax.dynamic_slice_in_dim(value_cache, start, key_block_rows, 0).reshape(
            key_block_rows, kv_count, HEAD
        )
        visible = (start + jnp.arange(key_block_rows, dtype=jnp.int32) < length)[None, None, :]
        return absorb(running, key_block, value_block, visible)

    rows_all = group_size * span_rows
    initial = (
        jnp.full((kv_count, rows_all), masked_score, jnp.float32),
        jnp.zeros((kv_count, rows_all), jnp.float32),
        jnp.zeros((kv_count, rows_all, HEAD), jnp.float32),
    )
    running = lax.fori_loop(0, block_count, cache_step, initial)
    visible = (jnp.arange(span_rows, dtype=jnp.int32)[None, :] <= token_of_row[:, None])[None]
    running = absorb(
        running,
        keys_fresh.reshape(span_rows, kv_count, HEAD),
        values_fresh.reshape(span_rows, kv_count, HEAD),
        visible,
    )
    result = running[2] / running[1][:, :, None]
    result = result.reshape(kv_count, group_size, span_rows, HEAD).transpose(2, 0, 1, 3)
    return result.reshape(span_rows, kv_count * group_size * HEAD).astype(jnp.bfloat16)


def on_device(queries, keys_new, values_new, caches, lengths, moving, destination, out_weight):
    replicas = lax.axis_size("rep")
    own_index = lax.axis_index("rep")
    slot_count = caches.shape[0]
    cache_rows = caches.shape[2]
    width_local = caches.shape[3]
    piece_rows = cache_rows // replicas
    leaving_slot = moving[own_index]
    leaving = lax.dynamic_index_in_dim(caches, leaving_slot, 0, keepdims=False)
    spread = lax.all_to_all(leaving, "rep", split_axis=1, concat_axis=1, tiled=True)
    source_of = jnp.argsort(destination)
    gathered_pieces = spread.reshape(2, replicas, piece_rows, width_local)
    ordered = jnp.take(gathered_pieces, source_of, axis=1).reshape(2, cache_rows, width_local)
    arrived = lax.all_to_all(ordered, "rep", split_axis=1, concat_axis=1, tiled=True)
    anchor = source_of[own_index]
    incoming_length = lengths[anchor, moving[anchor]]
    updated = lax.dynamic_update_index_in_dim(caches, arrived, leaving_slot, 0)
    own_lengths = lengths[own_index]
    held_lengths = jnp.where(jnp.arange(slot_count) == leaving_slot, incoming_length, own_lengths)
    span_rows = queries.shape[0] // slot_count
    results = []
    for slot_number in range(slot_count):
        length = held_lengths[slot_number]
        block_count = cache_rows // key_block_rows
        lower = slot_number * span_rows
        results.append(
            attend(
                queries[lower : lower + span_rows],
                updated[slot_number, 0],
                updated[slot_number, 1],
                length,
                keys_new[lower : lower + span_rows],
                values_new[lower : lower + span_rows],
                block_count,
            )
        )
    attended = jnp.concatenate(results, axis=0)
    partial_value = jnp.dot(attended, out_weight, preferred_element_type=jnp.float32)
    mixed = lax.psum_scatter(
        partial_value.astype(jnp.bfloat16), "tp", scatter_dimension=1, tiled=True
    )
    return (mixed, updated)


def solution(mesh):
    in_specs = (
        P("rep", "tp"),
        P("rep", "tp"),
        P("rep", "tp"),
        P("rep", None, None, "tp"),
        P(),
        P(),
        P(),
        P("tp", None),
    )
    out_specs = (P("rep", "tp"), P("rep", None, None, "tp"))
    return jax.shard_map(
        on_device, mesh=mesh, in_specs=in_specs, out_specs=out_specs, check_vma=False
    )
```

profile of v0, /device:TPU:0, one launch (start us, length us, event | category | flops | bytes accessed | tf_op | source)
XLA Modules:
  0.0 365.8 jit_solution(7094466064213119870)
XLA Ops:
  7.2 7.3 %copy.152 = bf16[2,2,4096,256]{3,2,1,0:T(8,128)(2,1)} copy(bf16[2,2,4096,256]{3,2,1,0:T(8,128)(2,1)} %param.15) | data formatting | bytes 16777216
  20.5 2.5 constant_dynamic-slice_fusion.4
  23.0 27.2 %copy.117 = bf16[1,2,4096,256]{3,1,2,0:T(2,128)(2,1)} copy(bf16[1,2,4096,256]{3,2,1,0:T(8,128)(2,1)S(1)} %constant_dynamic-slice_fusion.4) | data formatting | bytes 8388608 | tf_op jit(solution)/shard_map/jit(dynamic_index_in_dim)/dynamic_slice | solution.py:77
  50.2 5.2 %all-to-all-start = ((bf16[2,4096,256]{2,0,1:T(2,128)(2,1)}), bf16[2,4096,256]{2,0,1:T(2,128)(2,1)}, u32[]{:S(2)}, u32[]{:S(2)}) async-start(bf16[2,4096,256]{2,0,1:T(2,128)(2,1)} %bitcast.118), calls=%async_computation | async-start | bytes 8388608 | tf_op jit(solution)/shard_map/all_to_all | solution.py:78
  55.5 49.1 %all-to-all-done = bf16[2,4096,256]{2,0,1:T(2,128)(2,1)} async-done(((bf16[2,4096,256]{2,0,1:T(2,128)(2,1)}), bf16[2,4096,256]{2,0,1:T(2,128)(2,1)}, u32[]{:S(2)}, u32[]{:S(2)}) %all-to-all-start) | async-done | bytes 4194336 | tf_op jit(solution)/shard_map/all_to_all | solution.py:78
  104.5 4.7 %copy.72 = bf16[2,4096,256]{2,1,0:T(8,128)(2,1)} copy(bf16[2,4096,256]{2,0,1:T(2,128)(2,1)} %all-to-all-done) | data formatting | bytes 8388608 | tf_op jit(solution)/shard_map/all_to_all | solution.py:78
  109.2 4.9 %gather_fusion = bf16[8,2,512,256]{3,2,1,0:T(8,128)(2,1)} fusion(bf16[2,8,512,256]{3,2,1,0:T(8,128)(2,1)} %bitcast.119, s32[1024]{0:T(1024)S(1)} %pad_clamp_fusion), kind=kCustom, calls=%fused_computation | custom fusion | bytes 8388640 | tf_op jit(solution)/shard_map/jit(_take)/gather | solution.py:81
  114.2 2.5 copy.73
  117.7 27.2 %copy.74 = bf16[2,4096,256]{2,0,1:T(2,128)(2,1)} copy(bf16[2,4096,256]{2,1,0:T(8,128)(2,1)S(1)} %bitcast_select_fusion) | data formatting | bytes 8388608 | tf_op jit(solution)/shard_map/jit(_take)/select_n | solution.py:81
  144.9 4.7 %all-to-all-start.1 = ((bf16[2,4096,256]{2,0,1:T(2,128)(2,1)}), bf16[2,4096,256]{2,0,1:T(2,128)(2,1)}, u32[]{:S(2)}, u32[]{:S(2)}) async-start(bf16[2,4096,256]{2,0,1:T(2,128)(2,1)} %copy.74), calls=%async_computation.1 | async-start | bytes 8388608 | tf_op jit(solution)/shard_map/all_to_all | solution.py:82
  159.0 39.7 %all-to-all-done.1 = bf16[2,4096,256]{2,0,1:T(2,128)(2,1)} async-done(((bf16[2,4096,256]{2,0,1:T(2,128)(2,1)}), bf16[2,4096,256]{2,0,1:T(2,128)(2,1)}, u32[]{:S(2)}, u32[]{:S(2)}) %all-to-all-start.1) | async-done | bytes 4194336 | tf_op jit(solution)/shard_map/all_to_all | solution.py:82
  198.6 4.7 %copy_dynamic-update-slice_fusion = bf16[2,2,4096,256]{3,2,1,0:T(8,128)(2,1)} fusion(bf16[2,2,4096,256]{3,2,1,0:T(8,128)(2,1)} %copy.152, s32[]{:T(128)S(6)} %select_n.120, bf16[1,2,4096,256]{3,1,2,0:T(2,128)(2,1)} %bitcast.9), kind=kLoop, calls=%fused_computation.53 | loop fusion | bytes 8388612 | tf_op jit(solution)/shard_map/jit(dynamic_update_index_in_dim)/dynamic_update_slice | solution.py:85
  203.4 5.9 %slice_bitcast_fusion.2 = (bf16[4096,256]{1,0:T(8,128)(2,1)}, bf16[4096,256]{1,0:T(8,128)(2,1)}, bf16[4096,256]{1,0:T(8,128)(2,1)}, bf16[4096,256]{1,0:T(8,128)(2,1)}) fusion(bf16[2,2,4096,256]{3,2,1,0:T(8,128)(2,1)} %copy_dynamic-update-slice_fusion), kind=kLoop, calls=%fused_computation.57 | loop fusion | bytes 16777216 | tf_op jit(solution)/shard_map/squeeze | solution.py:98
  209.3 47.3 %while.36 = (s32[]{:T(128)}, f32[2,512]{1,0:T(2,128)S(1)}, f32[2,512]{1,0:T(2,128)S(1)}, f32[2,512,128]{2,1,0:T(8,128)}, s32[]{:T(128)}, /*index=5*/bf16[4096,25...) while((s32[]{:T(128)}, f32[2,512]{1,0:T(2,128)S(1)}, ...), condition=%wide.region_4.5_spmd.clone, body=%wide.region_1.4_spmd.clone.sunk | while | flops 275650560 | bytes 10291387 | solution.py:56
  212.5 1.8 convolution_add_fusion.6
  217.5 2.8 convolution_add_fusion.6
  223.6 2.8 convolution_add_fusion.6
  229.6 2.8 convolution_add_fusion.6
  235.7 2.8 convolution_add_fusion.6
  241.7 2.8 convolution_add_fusion.6
  247.8 2.8 convolution_add_fusion.6
  253.8 2.8 convolution_add_fusion.6
  256.7 47.2 %while.37 = (s32[]{:T(128)}, f32[2,512]{1,0:T(2,128)S(1)}, f32[2,512]{1,0:T(2,128)S(1)}, f32[2,512,128]{2,1,0:T(8,128)}, s32[]{:T(128)}, /*index=5*/bf16[4096,25...) while((s32[]{:T(128)}, f32[2,512]{1,0:T(2,128)S(1)}, ...), condition=%wide.region_10.11_spmd.clone, body=%wide.region_7.10_spmd.clone.sunk | while | flops 275650560 | bytes 10291387 | solution.py:56
  264.9 2.8 convolution_add_fusion.7
  270.9 2.8 convolution_add_fusion.7
  277.0 2.8 convolution_add_fusion.7
  283.0 2.8 convolution_add_fusion.7
  289.0 2.8 convolution_add_fusion.7
  295.0 2.8 convolution_add_fusion.7
  301.1 2.8 convolution_add_fusion.7
  308.0 7.1 %convolution_convert_fusion = bf16[256,4096]{1,0:T(8,128)(2,1)} fusion(bf16[1024,4096]{1,0:T(8,128)(2,1)} %param.19, bf16[128,1024]{0,1:T(8,128)(2,1)S(1)} %bitcast.128, bf16[128,1024]{0,1:T(8,128)(2,1)S(1)} %bitcast.127), kind=kOutput, calls=%fused_computation.51 | convolution fusion | flops 2149580800 | bytes 11010048 | tf_op jit(solution)/shard_map/dot_general | solution.py:106
  315.1 43.9 %reduce-scatter.2.cloned.1.call-done = bf16[256,1024]{1,0:T(8,128)(2,1)} async-done(((bf16[256,4096]{1,0:T(8,128)(2,1)}), bf16[256,1024]{1,0:T(8,128)(2,1)}) %reduce-scatter.2.cloned.1.call-update) | async-done | bytes 524304 | tf_op jit(solution)/shard_map/reduce_scatter | solution.py:107
  (208 shorter events, 66.9 us)
Async XLA Ops:
  7.2 10.8 %copy-start.6 = (s32[8]{0:T(128)S(1)}, s32[8]{0:T(128)}, u32[]{:S(2)}) copy-start(s32[8]{0:T(128)} %param.17) | copy-start | bytes 100
  7.2 7.3 %copy-start.7 = (s32[8]{0:T(128)S(1)}, s32[8]{0:T(128)}, u32[]{:S(2)}) copy-start(s32[8]{0:T(128)} %param.18) | copy-start | bytes 100
  50.2 54.4 %all-to-all-start = ((bf16[2,4096,256]{2,0,1:T(2,128)(2,1)}), bf16[2,4096,256]{2,0,1:T(2,128)(2,1)}, u32[]{:S(2)}, u32[]{:S(2)}) async-start(bf16[2,4096,256]{2,0,1:T(2,128)(2,1)} %bitcast.118), calls=%async_computation | async-start | bytes 8388608 | tf_op jit(solution)/shard_map/all_to_all | solution.py:78
  144.9 6.3 %copy-start.5 = (s32[8,2]{0,1:T(2,128)S(1)}, s32[8,2]{0,1:T(2,128)}, u32[]{:S(2)}) copy-start(s32[8,2]{0,1:T(2,128)} %param.16) | copy-start | bytes 196
  144.9 7.7 %copy-start.1 = (bf16[256,1024]{1,0:T(8,128)(2,1)S(1)}, bf16[256,1024]{1,0:T(8,128)(2,1)}, u32[]{:S(2)}) copy-start(bf16[256,1024]{1,0:T(8,128)(2,1)} %param.12) | copy-start | bytes 1572868
  144.9 53.8 %all-to-all-start.1 = ((bf16[2,4096,256]{2,0,1:T(2,128)(2,1)}), bf16[2,4096,256]{2,0,1:T(2,128)(2,1)}, u32[]{:S(2)}, u32[]{:S(2)}) async-start(bf16[2,4096,256]{2,0,1:T(2,128)(2,1)} %copy.74), calls=%async_computation.1 | async-start | bytes 8388608 | tf_op jit(solution)/shard_map/all_to_all | solution.py:82
  149.5 3.3 copy-start.2
  149.6 3.8 %copy-start.3 = (bf16[256,256]{1,0:T(8,128)(2,1)S(1)}, bf16[256,256]{1,0:T(8,128)(2,1)}, u32[]{:S(2)}) copy-start(bf16[256,256]{1,0:T(8,128)(2,1)} %param.14) | copy-start | bytes 393220
  149.6 209.4 %reduce-scatter.2.cloned.1.call-start = ((), (), s32[]{:S(2)}) async-start(), calls=%async_computation.3 | async-start | bytes 2621440 | tf_op jit(solution)/shard_map/reduce_scatter | solution.py:107
  256.7 47.3 %copy-start = (f32[2,512,128]{1,2,0:T(8,128)S(1)}, f32[2,512,128]{1,2,0:T(8,128)}, u32[]{:S(2)}) copy-start(f32[2,512,128]{1,2,0:T(8,128)} %get-tuple-element.461) | copy-start | bytes 1572868
  303.9 3.3 copy-start.4
  303.9 3.3 copy-start.8
Sparse Core Ops, SparseCore 0:
  315.2 43.7 reduce-scatter.1
where the time goes:
time: 368 us; the launch traced here: 366 us
  waiting for transfers between devices  133 us (36%)
  local copies, waits for them, and re-layouts  114 us (31%)
  matrix products  63.8 us (17%)
  other arithmetic  24.7 us (7%)
  between operations  20.1 us (5%)
  starting transfers between devices  10.1 us (3%)
    all_to_all x1, waiting for transfers between devices, on_device(): lax.all_to_all(leaving, 'rep', split_axis=1, concat_axis=1, tiled=True)  49.1 us
    dot_general x18, matrix products, absorb(): jnp.einsum('gqk,kgd->gqd', weights_block.astype(jnp.bfloat16), value_bloc...  45.6 us
    reduce_scatter x1, waiting for transfers between devices, on_device(): lax.psum_scatter(partial_value.astype(jnp.bfloat16), 'tp', scatter_dimens...  43.9 us
    all_to_all x1, waiting for transfers between devices, on_device(): lax.all_to_all(ordered, 'rep', split_axis=1, concat_axis=1, tiled=True)  39.7 us
    dynamic_slice x2, local copies, waits for them, and re-layouts, on_device(): leaving = lax.dynamic_index_in_dim(caches, leaving_slot, 0, keepdims=False)  29.7 us
    select_n x1, local copies, waits for them, and re-layouts, on_device(): jnp.take(gathered_pieces, source_of, axis=1)  27.2 us
    dynamic_slice x32, local copies, waits for them, and re-layouts, cache_step(): lax.dynamic_slice_in_dim(value_cache, start, key_block_rows, 0)  19.3 us
    dot_general x18, matrix products, absorb(): jnp.einsum('gqd,kgd->gqk', grouped, key_block, preferred_element_type=jnp...  11.1 us
  transfers between devices with their start and end apart: 3, of which 3 were waited for; matrix products, arithmetic and copies ran while one was open for 2% of the time, Pallas kernels for 0%

commit v1 on v0

--- a/solution.py
+++ b/solution.py
@@ -79,7 +79,12 @@
     source_of = jnp.argsort(destination)
     gathered_pieces = spread.reshape(2, replicas, piece_rows, width_local)
     ordered = jnp.take(gathered_pieces, source_of, axis=1).reshape(2, cache_rows, width_local)
-    arrived = lax.all_to_all(ordered, "rep", split_axis=1, concat_axis=1, tiled=True)
+    arrived = jnp.concatenate(
+        jax.lax.all_to_all(
+            jnp.stack(jnp.split(ordered, jax.lax.psum(1, "rep"), axis=1), axis=0), "rep", 0, 0
+        ),
+        axis=1,
+    )
     anchor = source_of[own_index]
     incoming_length = lengths[anchor, moving[anchor]]
     updated = lax.dynamic_update_index_in_dim(caches, arrived, leaving_slot, 0)

time: 368 us -> 347 us (0.943)
  local copies, waits for them, and re-layouts: 114 us -> 93.2 us
    select_n x1 -> x0, local copies, waits for them, and re-layouts: 27.2 us -> none  [on_device(): jnp.take(gathered_pieces, source_of, axis=1)]
    unnamed x25 -> x32, local copies, waits for them, and re-layouts: 9.12 us -> 15 us
where the time goes in v1:
time: 347 us; the launch traced here: 345 us
  waiting for transfers between devices  133 us (38%)
  local copies, waits for them, and re-layouts  93.2 us (27%)
  matrix products  63.8 us (18%)
  other arithmetic  24.6 us (7%)
  between operations  19.7 us (6%)
  starting transfers between devices  10.1 us (3%)
    all_to_all x1, waiting for transfers between devices, on_device(): lax.all_to_all(leaving, 'rep', split_axis=1, concat_axis=1, tiled=True)  49.1 us
    dot_general x18, matrix products, absorb(): jnp.einsum('gqk,kgd->gqd', weights_block.astype(jnp.bfloat16), value_bloc...  45.6 us
    reduce_scatter x1, waiting for transfers between devices, on_device(): lax.psum_scatter(partial_value.astype(jnp.bfloat16), 'tp', scatter_dimens...  43.9 us
    all_to_all x1, waiting for transfers between devices, on_device(): jax.lax.all_to_all(jnp.stack(jnp.split(ordered, jax.lax.psum(1, 'rep'), a...  40 us
    dynamic_slice x2, local copies, waits for them, and re-layouts, on_device(): leaving = lax.dynamic_index_in_dim(caches, leaving_slot, 0, keepdims=False)  29.7 us
    dynamic_slice x32, local copies, waits for them, and re-layouts, cache_step(): lax.dynamic_slice_in_dim(value_cache, start, key_block_rows, 0)  19.3 us
    unnamed x32, local copies, waits for them, and re-layouts  15 us
    dot_general x18, matrix products, absorb(): jnp.einsum('gqd,kgd->gqk', grouped, key_block, preferred_element_type=jnp...  11.1 us
  transfers between devices with their start and end apart: 3, of which 3 were waited for; matrix products, arithmetic and copies ran while one was open for 2% of the time, Pallas kernels for 0%

profile of v1, /device:TPU:0, one launch (start us, length us, event | category | flops | bytes accessed | tf_op | source)
XLA Modules:
  0.0 345.2 jit_solution(17953803184644193642)
XLA Ops:
  7.2 7.3 %copy.197 = bf16[2,2,4096,256]{3,2,1,0:T(8,128)(2,1)} copy(bf16[2,2,4096,256]{3,2,1,0:T(8,128)(2,1)} %param.15) | data formatting | bytes 16777216
  20.3 2.5 constant_dynamic-slice_fusion.4
  22.8 27.2 %copy.155 = bf16[1,2,4096,256]{3,1,2,0:T(2,128)(2,1)} copy(bf16[1,2,4096,256]{3,2,1,0:T(8,128)(2,1)S(1)} %constant_dynamic-slice_fusion.4) | data formatting | bytes 8388608 | tf_op jit(solution)/shard_map/jit(dynamic_index_in_dim)/dynamic_slice | solution.py:77
  50.0 5.2 %all-to-all-start = ((bf16[2,4096,256]{2,0,1:T(2,128)(2,1)}), bf16[2,4096,256]{2,0,1:T(2,128)(2,1)}, u32[]{:S(2)}, u32[]{:S(2)}) async-start(bf16[2,4096,256]{2,0,1:T(2,128)(2,1)} %bitcast.151), calls=%async_computation | async-start | bytes 8388608 | tf_op jit(solution)/shard_map/all_to_all | solution.py:78
  55.3 49.1 %all-to-all-done = bf16[2,4096,256]{2,0,1:T(2,128)(2,1)} async-done(((bf16[2,4096,256]{2,0,1:T(2,128)(2,1)}), bf16[2,4096,256]{2,0,1:T(2,128)(2,1)}, u32[]{:S(2)}, u32[]{:S(2)}) %all-to-all-start) | async-done | bytes 4194336 | tf_op jit(solution)/shard_map/all_to_all | solution.py:78
  104.4 4.7 %copy.112 = bf16[2,4096,256]{2,1,0:T(8,128)(2,1)} copy(bf16[2,4096,256]{2,0,1:T(2,128)(2,1)} %all-to-all-done) | data formatting | bytes 8388608 | tf_op jit(solution)/shard_map/all_to_all | solution.py:78
  109.1 4.9 %gather_fusion = bf16[8,2,512,256]{3,2,1,0:T(8,128)(2,1)} fusion(bf16[2,8,512,256]{3,2,1,0:T(8,128)(2,1)} %bitcast.153, s32[1024]{0:T(1024)S(1)} %pad_clamp_fusion), kind=kCustom, calls=%fused_computation | custom fusion | bytes 8388640 | tf_op jit(solution)/shard_map/jit(_take)/gather | solution.py:81
  114.0 2.5 copy.113
  124.2 4.7 %all-to-all-start.1 = ((bf16[8,2,512,256]{3,2,1,0:T(8,128)(2,1)}), bf16[8,2,512,256]{3,2,1,0:T(8,128)(2,1)}, u32[]{:S(2)}, u32[]{:S(2)}) async-start(bf16[8,2,512,256]{3,2,1,0:T(8,128)(2,1)} %fusion.36), calls=%async_computation.1 | async-start | bytes 8388608 | tf_op jit(solution)/shard_map/all_to_all | solution.py:83
  137.9 40.0 %all-to-all-done.1 = bf16[8,2,512,256]{3,2,1,0:T(8,128)(2,1)} async-done(((bf16[8,2,512,256]{3,2,1,0:T(8,128)(2,1)}), bf16[8,2,512,256]{3,2,1,0:T(8,128)(2,1)}, u32[]{:S(2)}, u32[]{:S(2)}) %all-to-all-start.1) | async-done | bytes 4194336 | tf_op jit(solution)/shard_map/all_to_all | solution.py:83
  178.0 2.5 copy.114
  180.4 2.3 constant_dynamic-update-slice_fusion
  182.7 5.9 %slice_bitcast_fusion.2 = (bf16[4096,256]{1,0:T(8,128)(2,1)}, bf16[4096,256]{1,0:T(8,128)(2,1)}, bf16[4096,256]{1,0:T(8,128)(2,1)}, bf16[4096,256]{1,0:T(8,128)(2,1)}) fusion(bf16[2,2,4096,256]{3,2,1,0:T(8,128)(2,1)} %constant_dynamic-update-slice_fusion), kind=kLoop, calls=%fused_computation.56 | loop fusion | bytes 16777216 | tf_op jit(solution)/shard_map/squeeze | solution.py:103
  188.7 47.3 %while.36 = (s32[]{:T(128)}, f32[2,512]{1,0:T(2,128)S(1)}, f32[2,512]{1,0:T(2,128)S(1)}, f32[2,512,128]{2,1,0:T(8,128)}, s32[]{:T(128)}, /*index=5*/bf16[4096,25...) while((s32[]{:T(128)}, f32[2,512]{1,0:T(2,128)S(1)}, ...), condition=%wide.region_4.5_spmd.clone, body=%wide.region_1.4_spmd.clone.sunk | while | flops 275650560 | bytes 10291387 | solution.py:56
  191.9 1.8 convolution_add_fusion.6
  196.9 2.8 convolution_add_fusion.6
  202.9 2.8 convolution_add_fusion.6
  209.0 2.8 convolution_add_fusion.6
  215.0 2.8 convolution_add_fusion.6
  221.1 2.8 convolution_add_fusion.6
  227.1 2.8 convolution_add_fusion.6
  233.2 2.8 convolution_add_fusion.6
  236.0 47.2 %while.37 = (s32[]{:T(128)}, f32[2,512]{1,0:T(2,128)S(1)}, f32[2,512]{1,0:T(2,128)S(1)}, f32[2,512,128]{2,1,0:T(8,128)}, s32[]{:T(128)}, /*index=5*/bf16[4096,25...) while((s32[]{:T(128)}, f32[2,512]{1,0:T(2,128)S(1)}, ...), condition=%wide.region_10.11_spmd.clone, body=%wide.region_7.10_spmd.clone.sunk | while | flops 275650560 | bytes 10291387 | solution.py:56
  244.2 2.8 convolution_add_fusion.7
  250.3 2.8 convolution_add_fusion.7
  256.3 2.8 convolution_add_fusion.7
  262.3 2.8 convolution_add_fusion.7
  268.4 2.8 convolution_add_fusion.7
  274.4 2.8 convolution_add_fusion.7
  280.4 2.8 convolution_add_fusion.7
  287.3 7.1 %convolution_convert_fusion = bf16[256,4096]{1,0:T(8,128)(2,1)} fusion(bf16[1024,4096]{1,0:T(8,128)(2,1)} %param.19, bf16[128,1024]{0,1:T(8,128)(2,1)S(1)} %bitcast.162, bf16[128,1024]{0,1:T(8,128)(2,1)S(1)} %bitcast.161), kind=kOutput, calls=%fused_computation.51 | convolution fusion | flops 2149580800 | bytes 11010048 | tf_op jit(solution)/shard_map/dot_general | solution.py:111
  294.4 43.9 %reduce-scatter.2.cloned.1.call-done = bf16[256,1024]{1,0:T(8,128)(2,1)} async-done(((bf16[256,4096]{1,0:T(8,128)(2,1)}), bf16[256,1024]{1,0:T(8,128)(2,1)}) %reduce-scatter.2.cloned.1.call-update) | async-done | bytes 524304 | tf_op jit(solution)/shard_map/reduce_scatter | solution.py:112
  (216 shorter events, 73.5 us)
Async XLA Ops:
  7.2 10.8 %copy-start.6 = (s32[8]{0:T(128)S(1)}, s32[8]{0:T(128)}, u32[]{:S(2)}) copy-start(s32[8]{0:T(128)} %param.17) | copy-start | bytes 100
  7.2 7.3 %copy-start.7 = (s32[8]{0:T(128)S(1)}, s32[8]{0:T(128)}, u32[]{:S(2)}) copy-start(s32[8]{0:T(128)} %param.18) | copy-start | bytes 100
  50.0 54.4 %all-to-all-start = ((bf16[2,4096,256]{2,0,1:T(2,128)(2,1)}), bf16[2,4096,256]{2,0,1:T(2,128)(2,1)}, u32[]{:S(2)}, u32[]{:S(2)}) async-start(bf16[2,4096,256]{2,0,1:T(2,128)(2,1)} %bitcast.151), calls=%async_computation | async-start | bytes 8388608 | tf_op jit(solution)/shard_map/all_to_all | solution.py:78
  124.2 6.1 %copy-start.5 = (s32[8,2]{0,1:T(2,128)S(1)}, s32[8,2]{0,1:T(2,128)}, u32[]{:S(2)}) copy-start(s32[8,2]{0,1:T(2,128)} %param.16) | copy-start | bytes 196
  124.2 7.4 %copy-start.1 = (bf16[256,1024]{1,0:T(8,128)(2,1)S(1)}, bf16[256,1024]{1,0:T(8,128)(2,1)}, u32[]{:S(2)}) copy-start(bf16[256,1024]{1,0:T(8,128)(2,1)} %param.12) | copy-start | bytes 1572868
  124.2 53.8 %all-to-all-start.1 = ((bf16[8,2,512,256]{3,2,1,0:T(8,128)(2,1)}), bf16[8,2,512,256]{3,2,1,0:T(8,128)(2,1)}, u32[]{:S(2)}, u32[]{:S(2)}) async-start(bf16[8,2,512,256]{3,2,1,0:T(8,128)(2,1)} %fusion.36), calls=%async_computation.1 | async-start | bytes 8388608 | tf_op jit(solution)/shard_map/all_to_all | solution.py:83
  128.9 3.0 copy-start.2
  128.9 3.5 %copy-start.3 = (bf16[256,256]{1,0:T(8,128)(2,1)S(1)}, bf16[256,256]{1,0:T(8,128)(2,1)}, u32[]{:S(2)}) copy-start(bf16[256,256]{1,0:T(8,128)(2,1)} %param.14) | copy-start | bytes 393220
  128.9 209.4 %reduce-scatter.2.cloned.1.call-start = ((), (), s32[]{:S(2)}) async-start(), calls=%async_computation.3 | async-start | bytes 2621440 | tf_op jit(solution)/shard_map/reduce_scatter | solution.py:112
  236.0 47.3 %copy-start = (f32[2,512,128]{1,2,0:T(8,128)S(1)}, f32[2,512,128]{1,2,0:T(8,128)}, u32[]{:S(2)}) copy-start(f32[2,512,128]{1,2,0:T(8,128)} %get-tuple-element.477) | copy-start | bytes 1572868
  283.3 3.3 copy-start.4
  283.3 3.3 copy-start.8
Sparse Core Ops, SparseCore 0:
  294.6 43.7 reduce-scatter.1
